TPU v7x, 32 devices: a whole 2x2x4 slice. The times are simulated.
32 devices in a mesh: row: 4 (over x, core), col: 8 (over z, y).
Axes of the slice: x: 2, y: 2, z: 4, core: 2. Of those that a mesh axis runs over, the one named last changes fastest.
Arguments:
- pooled: bfloat16 [2048, 1152], P(('row', 'col')), may hold values from -32 to 32
- hidden: bfloat16 [2048, 4304], P(('row', 'col')), may hold values from -6 to 6
- text: bfloat16 [2048, 1152], P(('row', 'col')), may hold values from -12 to 12
- weight: float32 [1152, 4304], P('col', 'row'), may hold values from -0.09375 to 0.09375
- row_moment: float32 [1152], P('col'), may hold values from 1e-07 to 1e-05
- col_moment: float32 [4304], P('row'), may hold values from 1e-07 to 1e-05
- log_scale: float32 [], replicated, may hold values from 4.2 to 4.8
- bias: float32 [], replicated, may hold values from -16 to -12
Outputs:
- update: float32 [1152, 4304], P('col', 'row')
- new_row: float32 [1152], P('col')
- new_col: float32 [4304], P('row')
- loss: float32 [], replicated
All inputs are finite; a program needn't handle non-finite values.
Results may differ from a plain program's by a relative error of at most 0.004.
Values may be sent and summed in bfloat16 or wider, within the bound.
A program may use at most 128 MiB of HBM per device.

v0:
```python
import jax
import jax.numpy as jnp
from jax import lax
from jax.sharding import PartitionSpec as P

D = 1152
FF = 4304
EPSILON = 1e-06
DECAY_RATE = 0.8
CLIP_LEVEL = 1.0
FLOOR_VALUE = 1e-30


def over_row_index(positions, column, tokens, columns):
    return (positions // tokens * columns + column) * tokens + positions % tokens


def over_col_index(positions, row_place, tokens, columns):
    return row_place * columns * tokens + positions


def pair_tile(images, image_ids, texts, text_ids, logit_scale, bias, batch_total):
    logits = logit_scale * jnp.dot(images, texts.T, preferred_element_type=jnp.float32) + bias
    label_sign = jnp.where(
        image_ids[:, None] == text_ids[None, :], jnp.float32(1.0), jnp.float32(-1.0)
    )
    loss_sum = jnp.sum(jax.nn.softplus(-label_sign * logits))
    grad_logits = (-label_sign * jax.nn.sigmoid(-label_sign * logits) / batch_total).astype(
        jnp.bfloat16
    )
    return (loss_sum, logit_scale * jnp.dot(grad_logits, texts, preferred_element_type=jnp.float32))


def per_device(pooled, hidden, text, weight, row_moment, col_moment, log_scale, bias):
    rows_count = lax.axis_size("row")
    cols_count = lax.axis_size("col")
    row_place = lax.axis_index("row")
    col_place = lax.axis_index("col")
    tokens = pooled.shape[0]
    batch_total = tokens * rows_count * cols_count
    split_hidden = lax.all_to_all(hidden, "row", split_axis=1, concat_axis=0, tiled=True)
    hidden_cols = split_hidden.shape[1]
    weight_half = weight.astype(jnp.bfloat16)
    grouped = split_hidden.reshape(rows_count, tokens, hidden_cols)
    hidden_all = lax.all_gather(grouped, "col", axis=1, tiled=True).reshape(
        batch_total, hidden_cols
    )
    partial_proj = lax.dot_general(
        weight_half, hidden_all, (((1,), (1,)), ((), ())), preferred_element_type=jnp.float32
    )
    summed = lax.psum_scatter(partial_proj, "row", scatter_dimension=1, tiled=True)
    projected = lax.all_to_all(summed, "col", split_axis=1, concat_axis=0, tiled=True).T
    mixed_rows = pooled.astype(jnp.float32) + projected
    length = jnp.sqrt(jnp.sum(mixed_rows * mixed_rows, axis=1, keepdims=True) + EPSILON)
    image_unit = mixed_rows / length
    images = image_unit.astype(jnp.bfloat16)
    text_float = text.astype(jnp.float32)
    text_units = (
        text_float / jnp.sqrt(jnp.sum(text_float * text_float, axis=1, keepdims=True) + EPSILON)
    ).astype(jnp.bfloat16)
    logit_scale = jnp.exp(log_scale)
    image_rows = lax.all_gather(images, "row", axis=0, tiled=True)
    image_ids = over_row_index(
        jnp.arange(image_rows.shape[0], dtype=jnp.int32), col_place, tokens, cols_count
    )
    piece = lax.all_gather(text_units, "col", axis=0, tiled=True)
    text_ids = over_col_index(
        jnp.arange(piece.shape[0], dtype=jnp.int32), row_place, tokens, cols_count
    )
    loss_local, unit_part = pair_tile(
        image_rows, image_ids, piece, text_ids, logit_scale, bias, batch_total
    )
    unit_grad = lax.psum_scatter(unit_part, "row", scatter_dimension=0, tiled=True)
    mixed_grad = (
        (unit_grad - image_unit * jnp.sum(image_unit * unit_grad, axis=1, keepdims=True)) / length
    ).astype(jnp.bfloat16)
    grad_cols = lax.all_to_all(mixed_grad.T, "col", split_axis=0, concat_axis=1, tiled=True)
    gradient = jnp.dot(
        lax.all_gather(grad_cols, "row", axis=1, tiled=True),
        hidden_all,
        preferred_element_type=jnp.float32,
    )
    squared = gradient * gradient + FLOOR_VALUE
    row_sum = lax.psum(jnp.sum(squared, axis=1), "row")
    col_sum = lax.psum(jnp.sum(squared, axis=0), "col")
    new_row = DECAY_RATE * row_moment + (1.0 - DECAY_RATE) * row_sum / FF
    new_col = DECAY_RATE * col_moment + (1.0 - DECAY_RATE) * col_sum / D
    second = new_row[:, None] * new_col[None, :]
    raw_update = gradient / jnp.sqrt(second)
    loss_total = lax.psum(loss_local, ("row", "col"))
    update_total = lax.psum(jnp.sum(raw_update * raw_update), ("row", "col"))
    update_rms = jnp.sqrt(update_total / (D * FF))
    update = raw_update / jnp.maximum(1.0, update_rms / CLIP_LEVEL)
    loss = loss_total / batch_total
    return (update, new_row, new_col, loss)


def solution(mesh):
    return jax.shard_map(
        per_device,
        mesh=mesh,
        in_specs=(
            P(("row", "col"), None),
            P(("row", "col"), None),
            P(("row", "col"), None),
            P("col", "row"),
            P("col"),
            P("row"),
            P(),
            P(),
        ),
        out_specs=(P("col", "row"), P("col"), P("row"), P()),
        check_vma=False,
    )
```

profile of v0, /device:TPU:12, one launch (start us, length us, event | category | flops | bytes accessed | tf_op | source)
XLA Modules:
  0.0 324.7 jit_solution(10579943734243616240)
XLA Ops:
  7.2 0.0 all-gather.3.cloned.1.call-start
  7.2 1.5 all_to_all.40
  8.7 0.1 copy.22
  8.8 12.1 %all_to_all.54 = bf16[64,4,1076]{2,0,1:T(8,128)(2,1)S(1)} all-to-all(bf16[64,4,1076]{2,0,1:T(8,128)(2,1)S(1)} %copy.22), channel_id=1, replica_groups=mesh['row'=4,'col'=8] {'row'}, dimensions={1} | all-to-all | bytes 1101824 | tf_op jit(solution)/shard_map/all_to_all | solution.py:41
  20.9 1.3 copy.23
  22.1 0.0 all-gather.3.cloned.1.call-update
  22.2 0.0 reduce-scatter.3.cloned.1.call-start
  22.2 78.1 %all-gather.3.cloned.1.call-done = bf16[4,512,1076]{2,0,1:T(4,128)(2,1)} async-done(((bf16[4,64,1076]{2,0,1:T(4,128)(2,1)}), bf16[4,512,1076]{2,0,1:T(4,128)(2,1)}) %all-gather.3.cloned.1.call-update) | async-done | bytes 4407312 | tf_op jit(solution)/shard_map/all_gather | solution.py:45
  100.3 10.4 %copy.24 = bf16[4,512,1076]{1,0,2:T(4,128)(2,1)} copy(bf16[4,512,1076]{2,0,1:T(4,128)(2,1)} %all-gather.3.cloned.1.call-done) | data formatting | bytes 8814592 | tf_op jit(solution)/shard_map/all_gather | solution.py:45
  110.7 3.9 %pad = bf16[1080,4,512]{2,1,0:T(4,128)(2,1)S(1)} pad(bf16[1076,4,512]{2,1,0:T(4,128)(2,1)} %bitcast.38, bf16[]{:T(256)} %constant.79), padding=0_4x0_0x0_0 | pad | bytes 8830978
  114.6 0.0 copy-start.2
  114.6 1.9 copy.31
  116.5 2.0 copy-done
  118.5 2.2 fusion.6
  120.8 0.0 reduce-scatter.3.cloned.1.call-update
  120.8 0.0 all-gather.5.cloned.1.call-start
  120.9 0.8 copy-done.3
  121.7 0.1 fusion.8
  121.8 0.8 fusion.9
  122.6 0.0 all-gather.5.cloned.1.call-update
  122.6 23.8 %reduce-scatter.3.cloned.1.call-done = f32[144,512]{1,0:T(8,128)} async-done(((f32[144,2048]{1,0:T(8,128)}), f32[144,512]{1,0:T(8,128)}) %reduce-scatter.3.cloned.1.call-update) | async-done | bytes 294928 | tf_op jit(solution)/shard_map/reduce_scatter | solution.py:51
  146.4 2.0 copy.29
  148.3 6.1 %all-to-all-start.1 = ((f32[144,8,64]{0,2,1:T(8,128)}), f32[144,8,64]{0,2,1:T(8,128)S(1)}, u32[]{:S(2)}, u32[]{:S(2)}) async-start(f32[144,8,64]{0,2,1:T(8,128)} %bitcast.1), calls=%async_computation.2 | async-start | bytes 1048576 | tf_op jit(solution)/shard_map/all_to_all | solution.py:52
  155.8 14.4 %all-to-all-done.1 = f32[144,8,64]{0,2,1:T(8,128)S(1)} async-done(((f32[144,8,64]{0,2,1:T(8,128)}), f32[144,8,64]{0,2,1:T(8,128)S(1)}, u32[]{:S(2)}, u32[]{:S(2)}) %all-to-all-start.1) | async-done | bytes 294944 | tf_op jit(solution)/shard_map/all_to_all | solution.py:52
  170.2 0.3 copy.26
  170.5 0.2 all_to_all.46
  170.7 0.1 multiply_reduce_fusion.2
  170.9 0.1 fusion.26
  171.0 7.1 %all_gather.13 = bf16[256,1152]{1,0:T(8,128)(2,1)S(1)} all-gather(bf16[64,1152]{1,0:T(8,128)(2,1)S(1)} %fusion.26), channel_id=1, replica_groups=mesh['row'=4,'col'=8] {'row'}, dimensions={0}, use_global_device_ids=true | all-gather | bytes 737280 | tf_op jit(solution)/shard_map/all_gather | solution.py:62
  178.1 12.6 %all-gather.5.cloned.1.call-done = bf16[512,1152]{1,0:T(8,128)(2,1)} async-done(((bf16[64,1152]{1,0:T(8,128)(2,1)}), bf16[512,1152]{1,0:T(8,128)(2,1)}) %all-gather.5.cloned.1.call-update) | async-done | bytes 1179664 | tf_op jit(solution)/shard_map/all_gather | solution.py:66
  190.6 2.9 fusion.5
  193.5 1.6 convolution_multiply_fusion
  195.1 0.0 reduce-scatter.5.cloned.1.call-update
  195.1 26.1 %reduce-scatter.5.cloned.1.call-done = f32[64,1152]{1,0:T(8,128)} async-done(((f32[256,1152]{1,0:T(8,128)}), f32[64,1152]{1,0:T(8,128)}) %reduce-scatter.5.cloned.1.call-update) | async-done | bytes 294928 | tf_op jit(solution)/shard_map/reduce_scatter | solution.py:73
  221.2 1.2 multiply_reduce_fusion.1
  222.4 1.1 fusion.16
  223.5 0.4 all_to_all.47
  223.9 12.6 %all_to_all.55 = bf16[8,144,64]{1,2,0:T(8,128)(2,1)S(1)} all-to-all(bf16[8,144,64]{1,2,0:T(8,128)(2,1)S(1)} %copy.27), channel_id=1, replica_groups=mesh['row'=4,'col'=8] {'col'}, dimensions={0} | all-to-all | bytes 294912 | tf_op jit(solution)/shard_map/all_to_all | solution.py:77
  236.5 0.1 copy.30
  236.6 6.7 %all_gather.15 = bf16[144,2048]{1,0:T(8,128)(2,1)S(1)} all-gather(bf16[144,512]{1,0:T(8,128)(2,1)S(1)} %copy.30), channel_id=1, replica_groups=mesh['row'=4,'col'=8] {'row'}, dimensions={1}, use_global_device_ids=true | all-gather | bytes 737280 | tf_op jit(solution)/shard_map/all_gather | solution.py:79
  243.3 4.1 %fusion.3 = (f32[144]{0:T(256)S(1)}, f32[1076]{0:T(1024)S(1)}, f32[144,1076]{1,0:T(8,128)S(1)}) fusion(bf16[144,2048]{1,0:T(8,128)(2,1)S(1)} %all_gather.15, bf16[2048,1076]{0,1:T(8,128)(2,1)} %bitcast.36), kind=kOutput, calls=%fused_computation.9 | convolution fusion | flops 635269184 | bytes 5621776 | tf_op jit(solution)/shard_map/dot_general | solution.py:78
  247.3 16.7 %psum.29 = f32[1076]{0:T(1024)S(1)} all-reduce(f32[1076]{0:T(1024)S(1)} %get-tuple-element.5), channel_id=1, replica_groups=mesh['row'=4,'col'=8] {'col'}, use_global_device_ids=true, to_apply=%region_8.9 | all-reduce | flops 1076 | bytes 8608 | tf_op jit(solution)/shard_map/psum | solution.py:85
  264.0 5.7 %psum.28 = f32[144]{0:T(256)S(1)} all-reduce(f32[144]{0:T(256)S(1)} %get-tuple-element.4), channel_id=1, replica_groups=mesh['row'=4,'col'=8] {'row'}, use_global_device_ids=true, to_apply=%region_6.7 | all-reduce | flops 144 | bytes 1152 | tf_op jit(solution)/shard_map/psum | solution.py:84
  269.7 0.0 copy-start.4
  269.7 0.0 copy-start.5
  269.7 0.9 multiply_reduce_fusion
  270.7 44.0 %all-reduce = (f32[]{:T(128)}, f32[]{:T(128)}) all-reduce(f32[]{:T(128)} %multiply_reduce_fusion, f32[]{:T(128)} %get-tuple-element.9), channel_id=1, replica_groups=mesh['row'=4,'col'=8] {'row','col'}, use_global_device_ids=true, to_apply=%region_10.11 | all-reduce | flops 2 | bytes 16 | tf_op jit(solution)/shard_map/psum | solution.py:91
  315.4 1.0 fusion.4
  (21 shorter events, 0.1 us)
Async XLA Ops:
  7.2 93.2 %all-gather.3.cloned.1.call-start = ((), (), s32[]{:S(2)}) async-start(), calls=%async_computation.5 | async-start | bytes 5308416 | tf_op jit(solution)/shard_map/all_gather | solution.py:45
  22.2 124.2 %reduce-scatter.3.cloned.1.call-start = ((), (), s32[]{:S(2)}) async-start(), calls=%async_computation.6 | async-start | bytes 1474560 | tf_op jit(solution)/shard_map/reduce_scatter | solution.py:51
  114.6 3.9 %copy-start.2 = (f32[144,1076]{1,0:T(8,128)S(1)}, f32[144,1076]{1,0:T(8,128)}, u32[]{:S(2)}) copy-start(f32[144,1076]{1,0:T(8,128)} %param.11) | copy-start | bytes 1859332
  116.5 2.0 copy-start
  120.8 0.9 copy-start.3
  120.8 69.8 %all-gather.5.cloned.1.call-start = ((), (), s32[]{:S(2)}) async-start(), calls=%async_computation.7 | async-start | bytes 1327104 | tf_op jit(solution)/shard_map/all_gather | solution.py:66
  148.3 21.8 %all-to-all-start.1 = ((f32[144,8,64]{0,2,1:T(8,128)}), f32[144,8,64]{0,2,1:T(8,128)S(1)}, u32[]{:S(2)}, u32[]{:S(2)}) async-start(f32[144,8,64]{0,2,1:T(8,128)} %bitcast.1), calls=%async_computation.2 | async-start | bytes 1048576 | tf_op jit(solution)/shard_map/all_to_all | solution.py:52
  154.4 16.3 %copy-start.1 = (bf16[64,1152]{1,0:T(8,128)(2,1)S(1)}, bf16[64,1152]{1,0:T(8,128)(2,1)}, u32[]{:S(2)}) copy-start(bf16[64,1152]{1,0:T(8,128)(2,1)} %param.8) | copy-start | bytes 442372
  154.4 66.8 %reduce-scatter.5.cloned.1.call-start = ((), (), s32[]{:S(2)}) async-start(), calls=%async_computation.8 | async-start | bytes 1474560 | tf_op jit(solution)/shard_map/reduce_scatter | solution.py:73
  190.6 2.9 copy-start.8
  243.3 26.4 %copy-start.6 = (f32[1076]{0:T(1024)S(1)}, f32[1076]{0:T(1024)}, u32[]{:S(2)}) copy-start(f32[1076]{0:T(1024)} %param.13) | copy-start | bytes 12916
  243.3 26.4 %copy-start.7 = (f32[144]{0:T(256)S(1)}, f32[144]{0:T(256)}, u32[]{:S(2)}) copy-start(f32[144]{0:T(256)} %param.12) | copy-start | bytes 1732
  269.7 47.3 %copy-start.4 = (f32[1076]{0:T(1024)}, f32[1076]{0:T(1024)S(1)}, u32[]{:S(2)}) copy-start(f32[1076]{0:T(1024)S(1)} %multiply_add_fusion.1) | copy-start | bytes 12916
  269.7 47.3 %copy-start.5 = (f32[144]{0:T(256)}, f32[144]{0:T(256)S(1)}, u32[]{:S(2)}) copy-start(f32[144]{0:T(256)S(1)} %multiply_add_fusion.2) | copy-start | bytes 1732
Sparse Core Ops, SparseCore 0:
  22.3 78.0 all-gather.2
  120.9 25.4 reduce-scatter.2
  148.6 41.9 all-gather.4
  195.3 25.9 reduce-scatter.4
where the time goes:
time: 326 us; the launch traced here: 325 us
  waiting for transfers between devices  155 us (48%)
  blocking collectives  105 us (32%)
  local copies, waits for them, and re-layouts  24.9 us (8%)
  between operations  17.8 us (5%)
  matrix products  10.8 us (3%)
  starting transfers between devices  6.18 us (2%)
  other arithmetic  5.36 us (2%)
    all_gather x1, waiting for transfers between devices, per_device(): lax.all_gather(grouped, 'col', axis=1, tiled=True)  78.1 us
    psum x1, blocking collectives, per_device(): update_total = lax.psum(jnp.sum(raw_update * raw_update), ('row', 'col'))  44 us
    reduce_scatter x1, waiting for transfers between devices, per_device(): lax.psum_scatter(unit_part, 'row', scatter_dimension=0, tiled=True)  26.1 us
    reduce_scatter x1, waiting for transfers between devices, per_device(): lax.psum_scatter(partial_proj, 'row', scatter_dimension=1, tiled=True)  23.8 us
    psum x1, blocking collectives, per_device(): col_sum = lax.psum(jnp.sum(squared, axis=0), 'col')  16.7 us
    all_to_all x1, waiting for transfers between devices, per_device(): lax.all_to_all(summed, 'col', split_axis=1, concat_axis=0, tiled=True)  14.4 us
    all_to_all x1, blocking collectives, per_device(): lax.all_to_all(mixed_grad.T, 'col', split_axis=0, concat_axis=1, tiled=True)  12.6 us
    all_gather x1, waiting for transfers between devices, per_device(): piece = lax.all_gather(text_units, 'col', axis=0, tiled=True)  12.6 us
  transfers between devices with their start and end apart: 5, of which 5 were waited for; matrix products, arithmetic and copies ran while one was open for 1% of the time, Pallas kernels for 0%

commit v1 on v0

--- a/solution.py
+++ b/solution.py
@@ -42,9 +42,12 @@
     hidden_cols = split_hidden.shape[1]
     weight_half = weight.astype(jnp.bfloat16)
     grouped = split_hidden.reshape(rows_count, tokens, hidden_cols)
-    hidden_all = lax.all_gather(grouped, "col", axis=1, tiled=True).reshape(
-        batch_total, hidden_cols
-    )
+
+    def values_supply_all(vals):
+        y_new = lax.all_gather(vals, "col")
+        return jnp.concatenate(y_new, axis=1)
+
+    hidden_all = values_supply_all(grouped).reshape(batch_total, hidden_cols)
     partial_proj = lax.dot_general(
         weight_half, hidden_all, (((1,), (1,)), ((), ())), preferred_element_type=jnp.float32
     )

time: 326 us -> 311 us (0.954)
  local copies, waits for them, and re-layouts: 24.9 us -> 10.4 us
    all_gather x1 -> x0, local copies, waits for them, and re-layouts: 10.4 us -> none  [per_device(): lax.all_gather(grouped, 'col', axis=1, tiled=True)]
    unnamed x20 -> x18, local copies, waits for them, and re-layouts: 8.66 us -> 2.98 us
where the time goes in v1:
time: 311 us
  waiting for transfers between devices  155 us (50%)
  blocking collectives  105 us (34%)
  between operations  17.8 us (6%)
  matrix products  10.7 us (3%)
  local copies, waits for them, and re-layouts  10.4 us (3%)
  starting transfers between devices  6.15 us (2%)
  other arithmetic  5.35 us (2%)
    all_gather x1, waiting for transfers between devices, values_supply_all(): y_new = lax.all_gather(vals, 'col')  78.1 us
    psum x1, blocking collectives, per_device(): update_total = lax.psum(jnp.sum(raw_update * raw_update), ('row', 'col'))  44 us
    reduce_scatter x1, waiting for transfers between devices, per_device(): lax.psum_scatter(unit_part, 'row', scatter_dimension=0, tiled=True)  26.1 us
    reduce_scatter x1, waiting for transfers between devices, per_device(): lax.psum_scatter(partial_proj, 'row', scatter_dimension=1, tiled=True)  23.8 us
    psum x1, blocking collectives, per_device(): col_sum = lax.psum(jnp.sum(squared, axis=0), 'col')  16.7 us
    all_to_all x1, waiting for transfers between devices, per_device(): lax.all_to_all(summed, 'col', split_axis=1, concat_axis=0, tiled=True)  14.4 us
    all_to_all x1, blocking collectives, per_device(): lax.all_to_all(hidden, 'row', split_axis=1, concat_axis=0, tiled=True)  12.6 us
    all_to_all x1, blocking collectives, per_device(): lax.all_to_all(mixed_grad.T, 'col', split_axis=0, concat_axis=1, tiled=True)  12.6 us
  transfers between devices with their start and end apart: 5, of which 5 were waited for; matrix products, arithmetic and copies ran while one was open for 1% of the time, Pallas kernels for 0%

profile of v1, /device:TPU:12, one launch (start us, length us, event | category | flops | bytes accessed | tf_op | source)
XLA Modules:
  0.0 310.7 jit_solution(11505016949737498635)
XLA Ops:
  7.2 0.0 all-gather.6.cloned.1.call-start
  7.2 1.5 all_to_all.40
  8.7 0.1 copy.22
  8.8 12.6 %all_to_all.54 = bf16[64,4,1076]{2,0,1:T(8,128)(2,1)} all-to-all(bf16[64,4,1076]{2,0,1:T(8,128)(2,1)S(1)} %copy.22), channel_id=1, replica_groups=mesh['row'=4,'col'=8] {'row'}, dimensions={1} | all-to-all | bytes 1101824 | tf_op jit(solution)/shard_map/all_to_all | solution.py:41
  21.4 0.0 all-gather.6.cloned.1.call-update
  21.4 0.0 reduce-scatter.3.cloned.1.call-start
  21.5 78.1 %all-gather.6.cloned.1.call-done = bf16[32,64,1076]{2,1,0:T(8,128)(2,1)} async-done(((bf16[4,64,1076]{2,1,0:T(8,128)(2,1)}), bf16[32,64,1076]{2,1,0:T(8,128)(2,1)}) %all-gather.6.cloned.1.call-update) | async-done | bytes 4407312 | tf_op jit(solution)/shard_map/all_gather | solution.py:47
  99.6 2.8 copy.23
  102.5 0.0 copy-start
  102.5 2.1 copy-done
  104.6 0.0 copy-done.2
  104.6 2.7 fusion.6
  107.3 0.0 reduce-scatter.3.cloned.1.call-update
  107.3 0.0 all-gather.4.cloned.1.call-start
  107.4 0.8 copy-done.3
  108.2 0.1 fusion.8
  108.4 0.8 fusion.9
  109.1 0.0 all-gather.4.cloned.1.call-update
  109.2 23.8 %reduce-scatter.3.cloned.1.call-done = f32[144,512]{1,0:T(8,128)} async-done(((f32[144,2048]{1,0:T(8,128)}), f32[144,512]{1,0:T(8,128)}) %reduce-scatter.3.cloned.1.call-update) | async-done | bytes 294928 | tf_op jit(solution)/shard_map/reduce_scatter | solution.py:54
  132.9 2.0 copy.28
  134.9 6.0 %all-to-all-start.1 = ((f32[144,8,64]{0,2,1:T(8,128)}), f32[144,8,64]{0,2,1:T(8,128)S(1)}, u32[]{:S(2)}, u32[]{:S(2)}) async-start(f32[144,8,64]{0,2,1:T(8,128)} %bitcast.4), calls=%async_computation.2 | async-start | bytes 1048576 | tf_op jit(solution)/shard_map/all_to_all | solution.py:55
  142.3 14.4 %all-to-all-done.1 = f32[144,8,64]{0,2,1:T(8,128)S(1)} async-done(((f32[144,8,64]{0,2,1:T(8,128)}), f32[144,8,64]{0,2,1:T(8,128)S(1)}, u32[]{:S(2)}, u32[]{:S(2)}) %all-to-all-start.1) | async-done | bytes 294944 | tf_op jit(solution)/shard_map/all_to_all | solution.py:55
  156.7 0.3 copy.25
  157.0 0.2 all_to_all.46
  157.3 0.0 copy-done.1
  157.3 0.1 multiply_reduce_fusion.2
  157.4 0.1 fusion.26
  157.5 7.1 %all_gather.13 = bf16[256,1152]{1,0:T(8,128)(2,1)S(1)} all-gather(bf16[64,1152]{1,0:T(8,128)(2,1)S(1)} %fusion.26), channel_id=1, replica_groups=mesh['row'=4,'col'=8] {'row'}, dimensions={0}, use_global_device_ids=true | all-gather | bytes 737280 | tf_op jit(solution)/shard_map/all_gather | solution.py:65
  164.6 12.6 %all-gather.4.cloned.1.call-done = bf16[512,1152]{1,0:T(8,128)(2,1)} async-done(((bf16[64,1152]{1,0:T(8,128)(2,1)}), bf16[512,1152]{1,0:T(8,128)(2,1)}) %all-gather.4.cloned.1.call-update) | async-done | bytes 1179664 | tf_op jit(solution)/shard_map/all_gather | solution.py:69
  177.2 2.9 fusion.5
  180.0 1.7 convolution_multiply_fusion
  181.7 0.0 reduce-scatter.5.cloned.1.call-update
  181.7 26.1 %reduce-scatter.5.cloned.1.call-done = f32[64,1152]{1,0:T(8,128)} async-done(((f32[256,1152]{1,0:T(8,128)}), f32[64,1152]{1,0:T(8,128)}) %reduce-scatter.5.cloned.1.call-update) | async-done | bytes 294928 | tf_op jit(solution)/shard_map/reduce_scatter | solution.py:76
  207.8 1.2 multiply_reduce_fusion.1
  209.0 1.1 fusion.16
  210.1 0.4 all_to_all.47
  210.5 12.6 %all_to_all.55 = bf16[8,144,64]{1,2,0:T(8,128)(2,1)S(1)} all-to-all(bf16[8,144,64]{1,2,0:T(8,128)(2,1)S(1)} %copy.26), channel_id=1, replica_groups=mesh['row'=4,'col'=8] {'col'}, dimensions={0} | all-to-all | bytes 294912 | tf_op jit(solution)/shard_map/all_to_all | solution.py:80
  223.1 0.1 copy.29
  223.2 6.7 %all_gather.15 = bf16[144,2048]{1,0:T(8,128)(2,1)S(1)} all-gather(bf16[144,512]{1,0:T(8,128)(2,1)S(1)} %copy.29), channel_id=1, replica_groups=mesh['row'=4,'col'=8] {'row'}, dimensions={1}, use_global_device_ids=true | all-gather | bytes 737280 | tf_op jit(solution)/shard_map/all_gather | solution.py:82
  229.9 3.5 %fusion.3 = (f32[144]{0:T(256)S(1)}, f32[1076]{0:T(1024)S(1)}, f32[144,1076]{1,0:T(8,128)S(1)}) fusion(bf16[144,2048]{1,0:T(8,128)(2,1)S(1)} %all_gather.15, bf16[2048,1076]{1,0:T(8,128)(2,1)} %bitcast.35), kind=kOutput, calls=%fused_computation.9 | convolution fusion | flops 635269184 | bytes 5621776 | tf_op jit(solution)/shard_map/dot_general | solution.py:81
  233.4 16.7 %psum.29 = f32[1076]{0:T(1024)S(1)} all-reduce(f32[1076]{0:T(1024)S(1)} %get-tuple-element.5), channel_id=1, replica_groups=mesh['row'=4,'col'=8] {'col'}, use_global_device_ids=true, to_apply=%region_8.9 | all-reduce | flops 1076 | bytes 8608 | tf_op jit(solution)/shard_map/psum | solution.py:88
  250.0 5.7 %psum.28 = f32[144]{0:T(256)S(1)} all-reduce(f32[144]{0:T(256)S(1)} %get-tuple-element.4), channel_id=1, replica_groups=mesh['row'=4,'col'=8] {'row'}, use_global_device_ids=true, to_apply=%region_6.7 | all-reduce | flops 144 | bytes 1152 | tf_op jit(solution)/shard_map/psum | solution.py:87
  255.7 0.0 copy-done.6
  255.7 0.0 copy-start.4
  255.7 0.0 copy-start.5
  255.7 0.9 multiply_reduce_fusion
  256.7 44.0 %all-reduce = (f32[]{:T(128)}, f32[]{:T(128)}) all-reduce(f32[]{:T(128)} %multiply_reduce_fusion, f32[]{:T(128)} %get-tuple-element.9), channel_id=1, replica_groups=mesh['row'=4,'col'=8] {'row','col'}, use_global_device_ids=true, to_apply=%region_10.11 | all-reduce | flops 2 | bytes 16 | tf_op jit(solution)/shard_map/psum | solution.py:94
  301.4 1.0 fusion.4
  (18 shorter events, 0.1 us)
Async XLA Ops:
  7.2 92.5 %all-gather.6.cloned.1.call-start = ((), (), s32[]{:S(2)}) async-start(), calls=%async_computation.8 | async-start | bytes 5308416 | tf_op jit(solution)/shard_map/all_gather | solution.py:47
  21.4 111.5 %reduce-scatter.3.cloned.1.call-start = ((), (), s32[]{:S(2)}) async-start(), calls=%async_computation.5 | async-start | bytes 1474560 | tf_op jit(solution)/shard_map/reduce_scatter | solution.py:54
  99.6 5.0 %copy-start.2 = (f32[144,1076]{1,0:T(8,128)S(1)}, f32[144,1076]{1,0:T(8,128)}, u32[]{:S(2)}) copy-start(f32[144,1076]{1,0:T(8,128)} %param.11) | copy-start | bytes 1859332
  102.5 2.1 copy-start
  107.3 0.9 copy-start.3
  107.3 69.8 %all-gather.4.cloned.1.call-start = ((), (), s32[]{:S(2)}) async-start(), calls=%async_computation.6 | async-start | bytes 1327104 | tf_op jit(solution)/shard_map/all_gather | solution.py:69
  134.9 21.8 %all-to-all-start.1 = ((f32[144,8,64]{0,2,1:T(8,128)}), f32[144,8,64]{0,2,1:T(8,128)S(1)}, u32[]{:S(2)}, u32[]{:S(2)}) async-start(f32[144,8,64]{0,2,1:T(8,128)} %bitcast.4), calls=%async_computation.2 | async-start | bytes 1048576 | tf_op jit(solution)/shard_map/all_to_all | solution.py:55
  140.9 16.3 %copy-start.1 = (bf16[64,1152]{1,0:T(8,128)(2,1)S(1)}, bf16[64,1152]{1,0:T(8,128)(2,1)}, u32[]{:S(2)}) copy-start(bf16[64,1152]{1,0:T(8,128)(2,1)} %param.8) | copy-start | bytes 442372
  140.9 66.9 %reduce-scatter.5.cloned.1.call-start = ((), (), s32[]{:S(2)}) async-start(), calls=%async_computation.7 | async-start | bytes 1474560 | tf_op jit(solution)/shard_map/reduce_scatter | solution.py:76
  177.2 2.9 copy-start.8
  229.9 25.8 %copy-start.6 = (f32[1076]{0:T(1024)S(1)}, f32[1076]{0:T(1024)}, u32[]{:S(2)}) copy-start(f32[1076]{0:T(1024)} %param.13) | copy-start | bytes 12916
  229.9 25.8 %copy-start.7 = (f32[144]{0:T(256)S(1)}, f32[144]{0:T(256)}, u32[]{:S(2)}) copy-start(f32[144]{0:T(256)} %param.12) | copy-start | bytes 1732
  255.7 47.3 %copy-start.4 = (f32[1076]{0:T(1024)}, f32[1076]{0:T(1024)S(1)}, u32[]{:S(2)}) copy-start(f32[1076]{0:T(1024)S(1)} %multiply_add_fusion.1) | copy-start | bytes 12916
  255.7 47.3 %copy-start.5 = (f32[144]{0:T(256)}, f32[144]{0:T(256)S(1)}, u32[]{:S(2)}) copy-start(f32[144]{0:T(256)S(1)} %multiply_add_fusion.2) | copy-start | bytes 1732
Sparse Core Ops, SparseCore 0:
  21.6 78.0 all-gather.5
  107.5 25.4 reduce-scatter.2
  135.1 41.9 all-gather.3
  181.9 25.9 reduce-scatter.4
